TPU v7x, 32 devices: a whole 2x2x4 slice. The times are simulated.
32 devices in a mesh: row: 4 (over x, core), col: 8 (over z, y).
Axes of the slice: x: 2, y: 2, z: 4, core: 2. Of those that a mesh axis runs over, the one named last changes fastest.
Arguments:
- w_rec: bfloat16 [2, 4096, 4, 4096], P(None, 'row', None, 'col'), may hold values from -0.09375 to 0.09375
- w_in: bfloat16 [2, 4096, 4, 4096], P(None, 'row', None, 'col'), may hold values from -0.09375 to 0.09375
- gate_pre: float32 [2, 6, 64, 4, 4096], P(None, None, None, None, 'col'), may hold values from -8 to 8, as said below
- cells: float32 [2, 7, 64, 4096], P(None, None, None, 'col'), may hold values from -6 to 6
- layer_in: bfloat16 [2, 6, 64, 4096], P(None, None, None, 'row'), may hold values from -1 to 1
- h_prev: bfloat16 [2, 6, 64, 4096], P(None, None, None, 'row'), may hold values from -1 to 1
- top_grad: float32 [6, 64, 4096], P(None, None, 'col'), may hold values from -40 to 40
Outputs:
- w_rec_grad: bfloat16 [2, 4096, 4, 4096], P(None, 'row', None, 'col')
- w_in_grad: bfloat16 [2, 4096, 4, 4096], P(None, 'row', None, 'col')
- input_grad: float32 [6, 64, 4096], P(None, None, 'col')
Inputs may be any that keep to these rules, and one draw needn't show every extreme that they name: `gate_pre`: dimension 3 holds the input, forget, candidate and output gates in that order.
All inputs are finite; a program needn't handle non-finite values.
Results may differ from a plain program's by a relative error of at most 0.0051.
Values sent between devices are 32-bit elements; how exact they have to be, the bound alone decides.
No kernel may reach another device: no remote copies, remote signals or barrier semaphores. Data moves between devices by JAX's collectives and lax.ppermute only.
A program may use at most 128 MiB of HBM per device.

v0:
```python
import jax
import jax.numpy as jnp
from jax import lax
from jax.sharding import PartitionSpec as P

WIDTH = 4096
LAYERS = 2


def from_root(block, axis, owner):
    block = jnp.where(lax.axis_index(axis) == owner, block, jnp.zeros_like(block))
    return lax.psum(block, axis)


def cell_backward(preact, cell_prev, cell_now, hid_grad, cell_carry):
    in_gate = jax.nn.sigmoid(preact[:, 0])
    forget = jax.nn.sigmoid(preact[:, 1])
    cand_gate = jnp.tanh(preact[:, 2])
    out_gate = jax.nn.sigmoid(preact[:, 3])
    tanh_cell = jnp.tanh(cell_now)
    cell_grad = cell_carry + hid_grad * out_gate * (1.0 - tanh_cell * tanh_cell)
    grad_in = cell_grad * cand_gate * in_gate * (1.0 - in_gate)
    grad_forget = cell_grad * cell_prev * forget * (1.0 - forget)
    grad_cand = cell_grad * in_gate * (1.0 - cand_gate * cand_gate)
    grad_out = hid_grad * tanh_cell * out_gate * (1.0 - out_gate)
    gate_grads = jnp.stack([grad_in, grad_forget, grad_cand, grad_out], axis=1).astype(jnp.bfloat16)
    return (gate_grads, cell_grad * forget)


def contract_gates(gate_flat, weight_flat):
    return lax.dot_general(
        gate_flat, weight_flat, (((1,), (1,)), ((), ())), preferred_element_type=jnp.float32
    )


def own_block(total):
    ratio = lax.axis_size("col") // lax.axis_size("row")
    width = total.shape[-1] // ratio
    column = lax.axis_index("col")
    piece = lax.dynamic_slice_in_dim(total, column % ratio * width, width, total.ndim - 1)
    return (piece, column // ratio)


def wave_units(partial_value):
    piece, root = own_block(lax.psum(partial_value, "col"))
    return from_root(piece, "row", root)


def input_units(partial_value):
    piece, root = own_block(lax.psum(partial_value, "col"))
    return from_root(piece, "row", root)


def local(w_rec, w_in, gate_pre, cells, layer_in, h_prev, top_grad):
    layers = w_rec.shape[0]
    row_units = w_rec.shape[1]
    steps, batch, col_units = top_grad.shape
    rec_flats = [w_rec[layer].reshape(row_units, 4 * col_units) for layer in range(layers)]
    in_flats = [w_in[layer].reshape(row_units, 4 * col_units) for layer in range(layers)]
    gate_store = [None] * layers
    zeros = jnp.zeros((layers, batch, col_units), jnp.float32)
    empty = tuple(
        (jnp.zeros((steps, batch, 4, col_units), jnp.bfloat16) for layer in range(layers))
    )

    def diagonal_step(diagonal, carry):
        rec_carry, cell_carry, above, stores = carry
        partials = []
        dx_partials = []
        new_cells = []
        new_stores = []
        for layer in range(layers):
            depth = layers - 1 - layer
            step_idx = steps - 1 - diagonal + depth
            valid = (step_idx >= 0) & (step_idx < steps)
            clamped = jnp.clip(step_idx, 0, steps - 1).astype(jnp.int32)
            preact = lax.dynamic_index_in_dim(gate_pre[layer], clamped, 0, keepdims=False)
            cell_prev = lax.dynamic_index_in_dim(cells[layer], clamped, 0, keepdims=False)
            cell_now = lax.dynamic_index_in_dim(cells[layer], clamped + 1, 0, keepdims=False)
            if layer == layers - 1:
                outside = lax.dynamic_index_in_dim(top_grad, clamped, 0, keepdims=False)
            else:
                outside = above[layer]
            gate_grads, cell_next = cell_backward(
                preact, cell_prev, cell_now, outside + rec_carry[layer], cell_carry[layer]
            )
            gate_grads = jnp.where(valid, gate_grads, jnp.zeros_like(gate_grads))
            cell_next = jnp.where(valid, cell_next, jnp.zeros_like(cell_next))
            previous = lax.dynamic_index_in_dim(stores[layer], clamped, 0, keepdims=False)
            written = jnp.where(valid, gate_grads, previous)
            new_stores.append(lax.dynamic_update_index_in_dim(stores[layer], written, clamped, 0))
            gate_flat = gate_grads.reshape(batch, 4 * col_units)
            partials.append(contract_gates(gate_flat, rec_flats[layer]))
            if layer > 0:
                dx_partials.append(contract_gates(gate_flat, in_flats[layer]))
            new_cells.append(cell_next)
        units = wave_units(jnp.concatenate(partials + dx_partials, axis=0))
        rec_next = jnp.stack(
            [units[layer * batch : (layer + 1) * batch] for layer in range(layers)]
        )
        above_list = [units[layers * batch : (layers + 1) * batch]]
        above_next = jnp.stack(above_list + [jnp.zeros((batch, col_units), jnp.float32)])
        return (rec_next, jnp.stack(new_cells), above_next, tuple(new_stores))

    final = lax.fori_loop(0, steps + layers - 1, diagonal_step, (zeros, zeros, zeros, empty))
    for layer in range(layers):
        gate_store[layer] = final[3][layer].reshape(steps * batch, 4 * col_units)
    input_grad = input_units(contract_gates(gate_store[0], in_flats[0])).reshape(
        steps, batch, col_units
    )
    rec_grads = []
    in_grads = []
    partial_sums = []
    for layer in range(layers):
        raw_rec = lax.dot_general(
            h_prev[layer].reshape(steps * batch, row_units),
            gate_store[layer],
            (((0,), (0,)), ((), ())),
            preferred_element_type=jnp.float32,
        )
        raw_in = lax.dot_general(
            layer_in[layer].reshape(steps * batch, row_units),
            gate_store[layer],
            (((0,), (0,)), ((), ())),
            preferred_element_type=jnp.float32,
        )
        rec_grads.append(raw_rec)
        in_grads.append(raw_in)
        partial_sums.append(jnp.sum(raw_rec * raw_rec) + jnp.sum(raw_in * raw_in))
    totals = [lax.psum(partial_value, ("row", "col")) for partial_value in partial_sums]
    sumsq = totals[0]
    for extra in totals[1:]:
        sumsq = sumsq + extra
    scale = 1.0 / jnp.maximum(jnp.sqrt(sumsq / (8.0 * LAYERS * WIDTH * WIDTH)), 0.05)
    w_rec_grad = jnp.stack(
        [(rec_grads[layer] * scale).reshape(row_units, 4, col_units) for layer in range(layers)]
    ).astype(jnp.bfloat16)
    w_in_grad = jnp.stack(
        [(in_grads[layer] * scale).reshape(row_units, 4, col_units) for layer in range(layers)]
    ).astype(jnp.bfloat16)
    return (w_rec_grad, w_in_grad, input_grad)


def solution(mesh):
    placed = (
        P(None, "row", None, "col"),
        P(None, "row", None, "col"),
        P(None, None, None, None, "col"),
        P(None, None, None, "col"),
        P(None, None, None, "row"),
        P(None, None, None, "row"),
        P(None, None, "col"),
    )
    return jax.shard_map(
        local,
        mesh=mesh,
        in_specs=placed,
        out_specs=(P(None, "row", None, "col"), P(None, "row", None, "col"), P(None, None, "col")),
        check_vma=False,
    )
```

profile of v0, /device:TPU:0, one launch (start us, length us, event | category | flops | bytes accessed | tf_op | source)
XLA Modules:
  0.0 1127.2 jit_solution(5628223669936796487)
XLA Ops:
  8.0 2.8 fusion.50
  12.2 7.8 copy.17
  20.0 2.9 fusion.49
  23.0 3.4 copy.33
  26.3 3.4 copy.32
  29.8 2.9 fusion.48
  32.7 3.4 copy.37
  36.1 3.4 copy.34
  43.4 897.5 %while.24 = (s32[]{:T(128)}, f32[2,64,512]{2,1,0:T(8,128)S(1)}, f32[2,64,512]{2,1,0:T(8,128)S(1)}, f32[2,64,512]{2,1,0:T(8,128)}, bf16[6,64,4,512]{3,2,1,0:T(4,1...) while((s32[]{:T(128)}, f32[2,64,512]{2,1,0:T(8,128)S(1)}, ...), condition=%wide.region_3.4_spmd, body=%wide.region_0.3_spmd.sunk | while | flops 811958272 | bytes 109184224 | solution.py:105
  55.9 1.7 fusion.96
  57.6 3.6 fusion.95
  61.3 2.0 fusion.97
  73.1 75.5 %all-reduce.10.cloned.1.call-done = f32[192,1024]{1,0:T(8,128)} async-done(((f32[192,1024]{1,0:T(8,128)}), f32[192,1024]{1,0:T(8,128)}) %all-reduce.10.cloned.1.call-update) | async-done | bytes 786448 | tf_op jit(solution)/shard_map/while/body/eval_jaxpr/psum | solution.py:45
  148.6 1.8 dynamic-slice_select_fusion.3
  151.6 31.3 %all-reduce.12.cloned.1.call-done = f32[192,512]{1,0:T(8,128)} async-done(((f32[192,512]{1,0:T(8,128)}), f32[192,512]{1,0:T(8,128)}) %all-reduce.12.cloned.1.call-update) | async-done | bytes 393232 | tf_op jit(solution)/shard_map/while/body/eval_jaxpr/psum | solution.py:12
  186.4 3.6 fusion.95
  190.1 2.0 fusion.97
  201.9 72.8 %all-reduce.10.cloned.1.call-done = f32[192,1024]{1,0:T(8,128)} async-done(((f32[192,1024]{1,0:T(8,128)}), f32[192,1024]{1,0:T(8,128)}) %all-reduce.10.cloned.1.call-update) | async-done | bytes 786448 | tf_op jit(solution)/shard_map/while/body/eval_jaxpr/psum | solution.py:45
  274.7 1.8 dynamic-slice_select_fusion.3
  277.7 31.2 %all-reduce.12.cloned.1.call-done = f32[192,512]{1,0:T(8,128)} async-done(((f32[192,512]{1,0:T(8,128)}), f32[192,512]{1,0:T(8,128)}) %all-reduce.12.cloned.1.call-update) | async-done | bytes 393232 | tf_op jit(solution)/shard_map/while/body/eval_jaxpr/psum | solution.py:12
  312.4 3.6 fusion.95
  316.1 2.0 fusion.97
  327.9 72.8 %all-reduce.10.cloned.1.call-done = f32[192,1024]{1,0:T(8,128)} async-done(((f32[192,1024]{1,0:T(8,128)}), f32[192,1024]{1,0:T(8,128)}) %all-reduce.10.cloned.1.call-update) | async-done | bytes 786448 | tf_op jit(solution)/shard_map/while/body/eval_jaxpr/psum | solution.py:45
  400.7 1.8 dynamic-slice_select_fusion.3
  403.7 31.2 %all-reduce.12.cloned.1.call-done = f32[192,512]{1,0:T(8,128)} async-done(((f32[192,512]{1,0:T(8,128)}), f32[192,512]{1,0:T(8,128)}) %all-reduce.12.cloned.1.call-update) | async-done | bytes 393232 | tf_op jit(solution)/shard_map/while/body/eval_jaxpr/psum | solution.py:12
  436.7 1.7 fusion.96
  438.4 3.6 fusion.95
  442.1 2.0 fusion.97
  453.9 72.8 %all-reduce.10.cloned.1.call-done = f32[192,1024]{1,0:T(8,128)} async-done(((f32[192,1024]{1,0:T(8,128)}), f32[192,1024]{1,0:T(8,128)}) %all-reduce.10.cloned.1.call-update) | async-done | bytes 786448 | tf_op jit(solution)/shard_map/while/body/eval_jaxpr/psum | solution.py:45
  526.7 1.8 dynamic-slice_select_fusion.3
  529.7 31.3 %all-reduce.12.cloned.1.call-done = f32[192,512]{1,0:T(8,128)} async-done(((f32[192,512]{1,0:T(8,128)}), f32[192,512]{1,0:T(8,128)}) %all-reduce.12.cloned.1.call-update) | async-done | bytes 393232 | tf_op jit(solution)/shard_map/while/body/eval_jaxpr/psum | solution.py:12
  564.6 3.6 fusion.95
  568.3 2.0 fusion.97
  580.1 72.8 %all-reduce.10.cloned.1.call-done = f32[192,1024]{1,0:T(8,128)} async-done(((f32[192,1024]{1,0:T(8,128)}), f32[192,1024]{1,0:T(8,128)}) %all-reduce.10.cloned.1.call-update) | async-done | bytes 786448 | tf_op jit(solution)/shard_map/while/body/eval_jaxpr/psum | solution.py:45
  652.9 1.8 dynamic-slice_select_fusion.3
  655.9 31.1 %all-reduce.12.cloned.1.call-done = f32[192,512]{1,0:T(8,128)} async-done(((f32[192,512]{1,0:T(8,128)}), f32[192,512]{1,0:T(8,128)}) %all-reduce.12.cloned.1.call-update) | async-done | bytes 393232 | tf_op jit(solution)/shard_map/while/body/eval_jaxpr/psum | solution.py:12
  690.6 3.6 fusion.95
  694.3 2.0 fusion.97
  706.1 72.8 %all-reduce.10.cloned.1.call-done = f32[192,1024]{1,0:T(8,128)} async-done(((f32[192,1024]{1,0:T(8,128)}), f32[192,1024]{1,0:T(8,128)}) %all-reduce.10.cloned.1.call-update) | async-done | bytes 786448 | tf_op jit(solution)/shard_map/while/body/eval_jaxpr/psum | solution.py:45
  778.9 1.8 dynamic-slice_select_fusion.3
  781.9 31.1 %all-reduce.12.cloned.1.call-done = f32[192,512]{1,0:T(8,128)} async-done(((f32[192,512]{1,0:T(8,128)}), f32[192,512]{1,0:T(8,128)}) %all-reduce.12.cloned.1.call-update) | async-done | bytes 393232 | tf_op jit(solution)/shard_map/while/body/eval_jaxpr/psum | solution.py:12
  816.6 3.6 fusion.95
  820.3 2.0 fusion.97
  832.1 72.8 %all-reduce.10.cloned.1.call-done = f32[192,1024]{1,0:T(8,128)} async-done(((f32[192,1024]{1,0:T(8,128)}), f32[192,1024]{1,0:T(8,128)}) %all-reduce.10.cloned.1.call-update) | async-done | bytes 786448 | tf_op jit(solution)/shard_map/while/body/eval_jaxpr/psum | solution.py:45
  904.9 1.8 dynamic-slice_select_fusion.3
  907.9 31.1 %all-reduce.12.cloned.1.call-done = f32[192,512]{1,0:T(8,128)} async-done(((f32[192,512]{1,0:T(8,128)}), f32[192,512]{1,0:T(8,128)}) %all-reduce.12.cloned.1.call-update) | async-done | bytes 393232 | tf_op jit(solution)/shard_map/while/body/eval_jaxpr/psum | solution.py:12
  940.9 2.0 copy.35
  943.3 6.3 multiply_reduce_fusion
  949.7 6.5 multiply_reduce_fusion.1
  956.2 3.0 fusion.55
  959.2 6.3 multiply_reduce_fusion.2
  965.5 6.6 multiply_reduce_fusion.3
  974.7 40.9 %psum.62 = f32[]{:T(128)} all-reduce(f32[]{:T(128)S(6)} %add.481), channel_id=1, replica_groups=mesh['row'=4,'col'=8] {'row','col'}, use_global_device_ids=true, to_apply=%region_6.7 | all-reduce | flops 1 | bytes 8 | tf_op jit(solution)/shard_map/psum | solution.py:130
  1016.4 11.7 %multiply_convert_fusion.4 = (bf16[2048,1024]{1,0:T(8,128)(2,1)}, bf16[2048,1024]{1,0:T(8,128)(2,1)}) fusion(f32[2048,1024]{1,0:T(8,128)} %get-tuple-element.427, f32[]{:T(128)S(6)} %div.192, f32[2048,1024]{1,0:T(8,128)} %get-tuple-element.423), kind=kLoop, calls=%fused_computation.93 | loop fusion | flops 8388608 | bytes 25165828 | tf_op jit(solution)/shard_map/convert.27
  1028.1 11.6 %multiply_convert_fusion.6 = (bf16[2048,1024]{1,0:T(8,128)(2,1)}, bf16[2048,1024]{1,0:T(8,128)(2,1)}) fusion(f32[2048,1024]{1,0:T(8,128)} %get-tuple-element.425, f32[]{:T(128)S(6)} %div.192, f32[2048,1024]{1,0:T(8,128)} %get-tuple-element.421), kind=kLoop, calls=%fused_computation.95 | loop fusion | flops 8388608 | bytes 25165828 | tf_op jit(solution)/shard_map/convert.33
  1039.7 8.0 copy.21
  1047.7 8.0 copy.20
  1055.6 7.8 copy.23
  1063.5 7.9 copy.22
  1071.4 8.7 pad_maximum_fusion.3
  1080.0 2.1 dynamic-slice_select_fusion.1
  1082.1 8.7 pad_maximum_fusion.4
  1090.8 26.8 %all-reduce.8.cloned.1.call-done = f32[6,64,512]{2,1,0:T(8,128)} async-done(((f32[6,64,512]{2,1,0:T(8,128)}), f32[6,64,512]{2,1,0:T(8,128)}) %all-reduce.8.cloned.1.call-update) | async-done | bytes 786448 | tf_op jit(solution)/shard_map/psum | solution.py:12
  1117.6 2.1 copy.77
  (398 shorter events, 103.0 us)
Async XLA Ops:
  10.8 9.2 slice-start
  12.2 7.9 slice-start.1
  22.9 6.8 slice-start.2
  55.8 92.8 %all-reduce.10.cloned.1.call-start = ((), (), s32[]{:S(2)}) async-start(), calls=%async_computation.2 | async-start | bytes 1572864 | tf_op jit(solution)/shard_map/while/body/eval_jaxpr/psum | solution.py:45
  68.2 4.6 copy-start.11
  68.2 4.6 copy-start.12
  68.2 4.6 copy-start.4
  68.2 4.6 copy-start.6
  68.2 4.6 copy-start.8
  68.2 4.6 copy-start.10
  70.6 112.3 %all-reduce.12.cloned.1.call-start = ((), (), s32[]{:S(2)}) async-start(), calls=%async_computation.3 | async-start | bytes 786432 | tf_op jit(solution)/shard_map/while/body/eval_jaxpr/psum | solution.py:12
  184.7 90.0 %all-reduce.10.cloned.1.call-start = ((), (), s32[]{:S(2)}) async-start(), calls=%async_computation.2 | async-start | bytes 1572864 | tf_op jit(solution)/shard_map/while/body/eval_jaxpr/psum | solution.py:45
  197.0 4.6 copy-start.11
  197.0 4.6 copy-start.12
  197.1 4.6 copy-start.4
  197.1 4.6 copy-start.6
  197.1 4.6 copy-start.8
  197.1 4.6 copy-start.10
  199.5 109.4 %all-reduce.12.cloned.1.call-start = ((), (), s32[]{:S(2)}) async-start(), calls=%async_computation.3 | async-start | bytes 786432 | tf_op jit(solution)/shard_map/while/body/eval_jaxpr/psum | solution.py:12
  310.7 90.0 %all-reduce.10.cloned.1.call-start = ((), (), s32[]{:S(2)}) async-start(), calls=%async_computation.2 | async-start | bytes 1572864 | tf_op jit(solution)/shard_map/while/body/eval_jaxpr/psum | solution.py:45
  323.0 4.6 copy-start.11
  323.0 4.6 copy-start.12
  323.1 4.6 copy-start.4
  323.1 4.6 copy-start.6
  323.1 4.6 copy-start.8
  323.1 4.6 copy-start.10
  325.5 109.4 %all-reduce.12.cloned.1.call-start = ((), (), s32[]{:S(2)}) async-start(), calls=%async_computation.3 | async-start | bytes 786432 | tf_op jit(solution)/shard_map/while/body/eval_jaxpr/psum | solution.py:12
  436.7 90.0 %all-reduce.10.cloned.1.call-start = ((), (), s32[]{:S(2)}) async-start(), calls=%async_computation.2 | async-start | bytes 1572864 | tf_op jit(solution)/shard_map/while/body/eval_jaxpr/psum | solution.py:45
  449.0 4.6 copy-start.11
  449.0 4.6 copy-start.12
  449.1 4.6 copy-start.4
  449.1 4.6 copy-start.6
  449.1 4.6 copy-start.8
  449.1 4.6 copy-start.10
  451.5 109.6 %all-reduce.12.cloned.1.call-start = ((), (), s32[]{:S(2)}) async-start(), calls=%async_computation.3 | async-start | bytes 786432 | tf_op jit(solution)/shard_map/while/body/eval_jaxpr/psum | solution.py:12
  562.9 90.0 %all-reduce.10.cloned.1.call-start = ((), (), s32[]{:S(2)}) async-start(), calls=%async_computation.2 | async-start | bytes 1572864 | tf_op jit(solution)/shard_map/while/body/eval_jaxpr/psum | solution.py:45
  575.2 4.6 copy-start.11
  575.2 4.6 copy-start.12
  575.2 4.6 copy-start.4
  575.2 4.6 copy-start.6
  575.2 4.6 copy-start.8
  575.2 4.6 copy-start.10
  577.6 109.4 %all-reduce.12.cloned.1.call-start = ((), (), s32[]{:S(2)}) async-start(), calls=%async_computation.3 | async-start | bytes 786432 | tf_op jit(solution)/shard_map/while/body/eval_jaxpr/psum | solution.py:12
  688.9 90.0 %all-reduce.10.cloned.1.call-start = ((), (), s32[]{:S(2)}) async-start(), calls=%async_computation.2 | async-start | bytes 1572864 | tf_op jit(solution)/shard_map/while/body/eval_jaxpr/psum | solution.py:45
  701.2 4.6 copy-start.11
  701.2 4.6 copy-start.12
  701.2 4.6 copy-start.4
  701.2 4.6 copy-start.6
  701.2 4.6 copy-start.8
  701.2 4.6 copy-start.10
  703.6 109.4 %all-reduce.12.cloned.1.call-start = ((), (), s32[]{:S(2)}) async-start(), calls=%async_computation.3 | async-start | bytes 786432 | tf_op jit(solution)/shard_map/while/body/eval_jaxpr/psum | solution.py:12
  814.9 90.0 %all-reduce.10.cloned.1.call-start = ((), (), s32[]{:S(2)}) async-start(), calls=%async_computation.2 | async-start | bytes 1572864 | tf_op jit(solution)/shard_map/while/body/eval_jaxpr/psum | solution.py:45
  827.2 4.6 copy-start.11
  827.2 4.6 copy-start.12
  827.2 4.6 copy-start.4
  827.2 4.6 copy-start.6
  827.2 4.6 copy-start.8
  827.2 4.6 copy-start.10
  829.6 109.4 %all-reduce.12.cloned.1.call-start = ((), (), s32[]{:S(2)}) async-start(), calls=%async_computation.3 | async-start | bytes 786432 | tf_op jit(solution)/shard_map/while/body/eval_jaxpr/psum | solution.py:12
  940.9 139.2 %all-reduce.6.cloned.1.call-start = ((), (), s32[]{:S(2)}) async-start(), calls=%async_computation | async-start | bytes 3145728 | tf_op jit(solution)/shard_map/psum | solution.py:50
  943.3 6.4 copy-start.17
  949.7 6.5 copy-start.14
  959.2 6.3 copy-start.15
  974.7 142.9 %all-reduce.8.cloned.1.call-start = ((), (), s32[]{:S(2)}) async-start(), calls=%async_computation.1 | async-start | bytes 1572864 | tf_op jit(solution)/shard_map/psum | solution.py:12
  (54 other events, 96.0 us)
Sparse Core Ops, SparseCore 0:
  70.7 77.7 all-reduce.9
  150.9 31.9 all-reduce.11
  199.6 75.0 all-reduce.9
  276.9 31.9 all-reduce.11
  325.6 75.0 all-reduce.9
  402.9 31.9 all-reduce.11
  451.6 75.0 all-reduce.9
  529.1 31.9 all-reduce.11
  577.7 75.0 all-reduce.9
  655.1 31.9 all-reduce.11
  703.7 75.0 all-reduce.9
  781.1 31.9 all-reduce.11
  829.7 75.0 all-reduce.9
  907.1 31.9 all-reduce.11
Sparse Core Ops, SparseCore 1:
  974.7 89.5 all-reduce.5
  1082.2 35.3 all-reduce.7
where the time goes:
time: 1140 us; the launch traced here: 1130 us
  waiting for transfers between devices  758 us (66%)
  local copies, waits for them, and re-layouts  149 us (13%)
  other arithmetic  87.8 us (8%)
  matrix products  57.9 us (5%)
  blocking collectives  40.9 us (4%)
  between operations  19 us (2%)
  loops' own time  14.8 us (1%)
    psum x7, waiting for transfers between devices, wave_units(): piece, root = own_block(lax.psum(partial_value, 'col'))  512 us
    psum x8, waiting for transfers between devices, from_root(): return lax.psum(block, axis)  245 us
    psum x1, blocking collectives, local(): lax.psum(partial_value, ('row', 'col'))  40.9 us
    another operation x23, other arithmetic  33.1 us
    dot_general x22, matrix products, contract_gates(): lax.dot_general(gate_flat, weight_flat, (((1,), (1,)), ((), ())), preferr...  32.2 us
    slice x7, local copies, waits for them, and re-layouts, diagonal_step(): gate_pre[layer]  24.9 us
  transfers between devices with their start and end apart: 16, of which 15 were waited for; matrix products, arithmetic and copies ran while one was open for 9% of the time, Pallas kernels for 0%

commit v1 on v0

--- a/solution.py
+++ b/solution.py
@@ -9,7 +9,7 @@
 
 def from_root(block, axis, owner):
     block = jnp.where(lax.axis_index(axis) == owner, block, jnp.zeros_like(block))
-    return lax.psum(block, axis)
+    return jnp.sum(lax.all_gather(block, axis), axis=0)
 
 
 def cell_backward(preact, cell_prev, cell_now, hid_grad, cell_carry):

time: 1140 us -> 1080 us (0.947)
  waiting for transfers between devices: 758 us -> 698 us
  other arithmetic: 87.8 us -> 103 us
  loops' own time: 14.8 us -> 3 us
    psum x8 -> x0, waiting for transfers between devices: 245 us -> none  [from_root(): return lax.psum(block, axis)]
    all_gather x0 -> x8, waiting for transfers between devices: none -> 108 us  [from_root(): return jnp.sum(lax.all_gather(block, axis), axis=0)]
    psum x1, waiting for transfers between devices: 0.01 us -> 60.8 us  [input_units(): piece, root = own_block(lax.psum(partial_value, 'col'))]
    psum x7, waiting for transfers between devices: 512 us -> 529 us  [wave_units(): piece, root = own_block(lax.psum(partial_value, 'col'))]
    reduce_sum x0 -> x8, other arithmetic: none -> 14.4 us  [from_root(): return jnp.sum(lax.all_gather(block, axis), axis=0)]
    another operation x1, loops' own time: 14.8 us -> 3 us  [local(): lax.fori_loop(0, steps + layers - 1, diagonal_step, (zeros, zeros, zeros,...]
  transfers between devices with their start and end apart: 16 -> 16, of which waited for: 15 -> 15; matrix products, arithmetic and copies ran while one was open for 9% -> 12% of each run, Pallas kernels for 0% -> 0%
where the time goes in v1:
time: 1080 us; the launch traced here: 1070 us
  waiting for transfers between devices  698 us (65%)
  local copies, waits for them, and re-layouts  139 us (13%)
  other arithmetic  103 us (10%)
  matrix products  62.2 us (6%)
  blocking collectives  40.6 us (4%)
  between operations  18.7 us (2%)
    psum x7, waiting for transfers between devices, wave_units(): piece, root = own_block(lax.psum(partial_value, 'col'))  529 us
    all_gather x8, waiting for transfers between devices, from_root(): return jnp.sum(lax.all_gather(block, axis), axis=0)  108 us
    psum x1, waiting for transfers between devices, input_units(): piece, root = own_block(lax.psum(partial_value, 'col'))  60.8 us
    psum x1, blocking collectives, local(): lax.psum(partial_value, ('row', 'col'))  40.6 us
    dot_general x22, matrix products, contract_gates(): lax.dot_general(gate_flat, weight_flat, (((1,), (1,)), ((), ())), preferr...  34.5 us
    another operation x23, other arithmetic  33.2 us
    slice x7, local copies, waits for them, and re-layouts, diagonal_step(): gate_pre[layer]  24.9 us
  transfers between devices with their start and end apart: 16, of which 15 were waited for; matrix products, arithmetic and copies ran while one was open for 12% of the time, Pallas kernels for 0%

profile of v1, /device:TPU:0, one launch (start us, length us, event | category | flops | bytes accessed | tf_op | source)
XLA Modules:
  0.0 1065.7 jit_solution(11434142763579889043)
XLA Ops:
  8.0 7.5 copy.17
  15.5 2.9 fusion.49
  18.5 3.4 copy.33
  21.9 3.4 copy.32
  25.4 2.9 fusion.48
  28.3 3.3 copy.37
  31.6 3.4 copy.34
  38.9 796.1 %while.24 = (s32[]{:T(128)}, f32[2,64,512]{2,1,0:T(8,128)S(1)}, f32[2,64,512]{2,1,0:T(8,128)S(1)}, f32[2,64,512]{2,1,0:T(8,128)}, bf16[6,64,4,512]{3,2,1,0:T(4,1...) while((s32[]{:T(128)}, f32[2,64,512]{2,1,0:T(8,128)S(1)}, ...), condition=%wide.region_3.4_spmd, body=%wide.region_0.3_spmd.sunk | while | flops 812154880 | bytes 114689248 | solution.py:105
  39.4 1.7 fusion.96
  41.1 3.6 fusion.95
  44.8 2.0 fusion.97
  54.3 77.9 %all-reduce.6.cloned.1.call-done = f32[192,1024]{1,0:T(8,128)} async-done(((f32[192,1024]{1,0:T(8,128)}), f32[192,1024]{1,0:T(8,128)}) %all-reduce.6.cloned.1.call-update) | async-done | bytes 786448 | tf_op jit(solution)/shard_map/while/body/eval_jaxpr/psum | solution.py:45
  132.1 1.8 dynamic-slice_select_fusion.3
  137.5 15.6 %all-gather.9.cloned.1.call-done = f32[768,512]{1,0:T(8,128)} async-done(((f32[192,512]{1,0:T(8,128)}), f32[768,512]{1,0:T(8,128)}) %all-gather.9.cloned.1.call-update) | async-done | bytes 1572880 | tf_op jit(solution)/shard_map/while/body/eval_jaxpr/all_gather | solution.py:12
  155.6 1.7 fusion.96
  157.3 3.6 fusion.95
  161.0 2.0 fusion.97
  170.4 75.1 %all-reduce.6.cloned.1.call-done = f32[192,1024]{1,0:T(8,128)} async-done(((f32[192,1024]{1,0:T(8,128)}), f32[192,1024]{1,0:T(8,128)}) %all-reduce.6.cloned.1.call-update) | async-done | bytes 786448 | tf_op jit(solution)/shard_map/while/body/eval_jaxpr/psum | solution.py:45
  245.5 1.8 dynamic-slice_select_fusion.3
  250.9 15.4 %all-gather.9.cloned.1.call-done = f32[768,512]{1,0:T(8,128)} async-done(((f32[192,512]{1,0:T(8,128)}), f32[768,512]{1,0:T(8,128)}) %all-gather.9.cloned.1.call-update) | async-done | bytes 1572880 | tf_op jit(solution)/shard_map/while/body/eval_jaxpr/all_gather | solution.py:12
  270.5 3.6 fusion.95
  274.2 2.0 fusion.97
  283.6 75.1 %all-reduce.6.cloned.1.call-done = f32[192,1024]{1,0:T(8,128)} async-done(((f32[192,1024]{1,0:T(8,128)}), f32[192,1024]{1,0:T(8,128)}) %all-reduce.6.cloned.1.call-update) | async-done | bytes 786448 | tf_op jit(solution)/shard_map/while/body/eval_jaxpr/psum | solution.py:45
  358.8 1.8 dynamic-slice_select_fusion.3
  364.2 15.4 %all-gather.9.cloned.1.call-done = f32[768,512]{1,0:T(8,128)} async-done(((f32[192,512]{1,0:T(8,128)}), f32[768,512]{1,0:T(8,128)}) %all-gather.9.cloned.1.call-update) | async-done | bytes 1572880 | tf_op jit(solution)/shard_map/while/body/eval_jaxpr/all_gather | solution.py:12
  383.7 3.6 fusion.95
  387.4 2.0 fusion.97
  396.9 75.1 %all-reduce.6.cloned.1.call-done = f32[192,1024]{1,0:T(8,128)} async-done(((f32[192,1024]{1,0:T(8,128)}), f32[192,1024]{1,0:T(8,128)}) %all-reduce.6.cloned.1.call-update) | async-done | bytes 786448 | tf_op jit(solution)/shard_map/while/body/eval_jaxpr/psum | solution.py:45
  472.0 1.8 dynamic-slice_select_fusion.3
  477.4 15.5 %all-gather.9.cloned.1.call-done = f32[768,512]{1,0:T(8,128)} async-done(((f32[192,512]{1,0:T(8,128)}), f32[768,512]{1,0:T(8,128)}) %all-gather.9.cloned.1.call-update) | async-done | bytes 1572880 | tf_op jit(solution)/shard_map/while/body/eval_jaxpr/all_gather | solution.py:12
  497.1 3.6 fusion.95
  500.8 2.0 fusion.97
  510.2 75.1 %all-reduce.6.cloned.1.call-done = f32[192,1024]{1,0:T(8,128)} async-done(((f32[192,1024]{1,0:T(8,128)}), f32[192,1024]{1,0:T(8,128)}) %all-reduce.6.cloned.1.call-update) | async-done | bytes 786448 | tf_op jit(solution)/shard_map/while/body/eval_jaxpr/psum | solution.py:45
  585.4 1.8 dynamic-slice_select_fusion.3
  590.8 15.4 %all-gather.9.cloned.1.call-done = f32[768,512]{1,0:T(8,128)} async-done(((f32[192,512]{1,0:T(8,128)}), f32[768,512]{1,0:T(8,128)}) %all-gather.9.cloned.1.call-update) | async-done | bytes 1572880 | tf_op jit(solution)/shard_map/while/body/eval_jaxpr/all_gather | solution.py:12
  610.4 3.6 fusion.95
  614.1 2.0 fusion.97
  623.5 75.1 %all-reduce.6.cloned.1.call-done = f32[192,1024]{1,0:T(8,128)} async-done(((f32[192,1024]{1,0:T(8,128)}), f32[192,1024]{1,0:T(8,128)}) %all-reduce.6.cloned.1.call-update) | async-done | bytes 786448 | tf_op jit(solution)/shard_map/while/body/eval_jaxpr/psum | solution.py:45
  698.6 1.8 dynamic-slice_select_fusion.3
  704.0 15.4 %all-gather.9.cloned.1.call-done = f32[768,512]{1,0:T(8,128)} async-done(((f32[192,512]{1,0:T(8,128)}), f32[768,512]{1,0:T(8,128)}) %all-gather.9.cloned.1.call-update) | async-done | bytes 1572880 | tf_op jit(solution)/shard_map/while/body/eval_jaxpr/all_gather | solution.py:12
  723.6 3.6 fusion.95
  727.3 2.0 fusion.97
  736.7 75.1 %all-reduce.6.cloned.1.call-done = f32[192,1024]{1,0:T(8,128)} async-done(((f32[192,1024]{1,0:T(8,128)}), f32[192,1024]{1,0:T(8,128)}) %all-reduce.6.cloned.1.call-update) | async-done | bytes 786448 | tf_op jit(solution)/shard_map/while/body/eval_jaxpr/psum | solution.py:45
  811.9 1.8 dynamic-slice_select_fusion.3
  817.3 15.4 %all-gather.9.cloned.1.call-done = f32[768,512]{1,0:T(8,128)} async-done(((f32[192,512]{1,0:T(8,128)}), f32[768,512]{1,0:T(8,128)}) %all-gather.9.cloned.1.call-update) | async-done | bytes 1572880 | tf_op jit(solution)/shard_map/while/body/eval_jaxpr/all_gather | solution.py:12
  835.1 1.8 copy.35
  837.0 5.3 fusion.55
  845.8 1.8 copy.36
  847.7 7.5 multiply_reduce_fusion
  855.2 6.5 multiply_reduce_fusion.1
  862.9 7.4 multiply_reduce_fusion.2
  870.3 60.8 %all-reduce.4.cloned.1.call-done = f32[384,1024]{1,0:T(8,128)} async-done(((f32[384,1024]{1,0:T(8,128)}), f32[384,1024]{1,0:T(8,128)}) %all-reduce.4.cloned.1.call-update) | async-done | bytes 1572880 | tf_op jit(solution)/shard_map/psum | solution.py:50
  931.1 2.1 dynamic-slice_select_fusion.1
  933.2 6.4 multiply_reduce_fusion.3
  940.8 40.6 %psum.39 = f32[]{:T(128)} all-reduce(f32[]{:T(128)S(6)} %add.477), channel_id=1, replica_groups=mesh['row'=4,'col'=8] {'row','col'}, use_global_device_ids=true, to_apply=%region_6.7 | all-reduce | flops 1 | bytes 8 | tf_op jit(solution)/shard_map/psum | solution.py:130
  982.2 11.7 %multiply_convert_fusion.6 = (bf16[2048,1024]{1,0:T(8,128)(2,1)}, bf16[2048,1024]{1,0:T(8,128)(2,1)}) fusion(f32[2048,1024]{1,0:T(8,128)} %get-tuple-element.425, f32[]{:T(128)S(6)} %div.192, f32[2048,1024]{1,0:T(8,128)} %get-tuple-element.421), kind=kLoop, calls=%fused_computation.95 | loop fusion | flops 8388608 | bytes 25165828 | tf_op jit(solution)/shard_map/convert.33
  993.8 7.8 copy.21
  1001.6 7.8 copy.20
  1009.5 11.8 %multiply_convert_fusion.4 = (bf16[2048,1024]{1,0:T(8,128)(2,1)}, bf16[2048,1024]{1,0:T(8,128)(2,1)}) fusion(f32[2048,1024]{1,0:T(8,128)} %get-tuple-element.427, f32[]{:T(128)S(6)} %div.192, f32[2048,1024]{1,0:T(8,128)} %get-tuple-element.423), kind=kLoop, calls=%fused_computation.93 | loop fusion | flops 8388608 | bytes 25165828 | tf_op jit(solution)/shard_map/convert.27
  1021.3 7.8 copy.23
  1029.1 7.9 copy.22
  1037.0 10.7 %pad_maximum_fusion.3 = bf16[2,1024,4,512]{3,2,1,0:T(4,128)(2,1)} fusion(bf16[1,1024,4,512]{3,2,1,0:T(4,128)(2,1)} %copy.21, bf16[1,1024,4,512]{3,2,1,0:T(4,128)(2,1)} %copy.20), kind=kLoop, calls=%fused_computation.91 | loop fusion | flops 4194304 | bytes 16777216 | tf_op jit(solution)/shard_map/stack | solution.py:135
  1047.7 7.4 pad_maximum_fusion.4
  1055.1 3.2 reduce_sum.66
  (400 shorter events, 109.0 us)
Async XLA Ops:
  8.0 7.5 copy-start.15
  18.5 6.9 slice-start
  39.4 92.8 %all-reduce.6.cloned.1.call-start = ((), (), s32[]{:S(2)}) async-start(), calls=%async_computation.2 | async-start | bytes 1572864 | tf_op jit(solution)/shard_map/while/body/eval_jaxpr/psum | solution.py:45
  51.8 84.2 %copy-start.13 = (f32[1,64,512]{2,1,0:T(8,128)S(1)}, f32[1,64,512]{2,1,0:T(8,128)}, u32[]{:S(2)}) copy-start(f32[1,64,512]{2,1,0:T(8,128)} %get-tuple-element.548) | copy-start | bytes 393220 | tf_op jit(solution)/shard_map/while
  51.8 84.2 %copy-start.14 = (f32[1,64,512]{2,1,0:T(8,128)S(1)}, f32[1,64,512]{2,1,0:T(8,128)}, u32[]{:S(2)}) copy-start(f32[1,64,512]{2,1,0:T(8,128)} %get-tuple-element.549) | copy-start | bytes 393220 | tf_op jit(solution)/shard_map/while
  51.8 84.3 %copy-start.6 = (bf16[64,1,512]{2,0,1:T(8,128)(2,1)S(1)}, bf16[64,1,512]{2,0,1:T(8,128)(2,1)}, u32[]{:S(2)}) copy-start(bf16[64,1,512]{2,0,1:T(8,128)(2,1)} %copy-done.5) | copy-start | bytes 196612 | tf_op jit(solution)/shard_map/while
  51.8 84.3 %copy-start.8 = (bf16[64,1,512]{2,0,1:T(8,128)(2,1)S(1)}, bf16[64,1,512]{2,0,1:T(8,128)(2,1)}, u32[]{:S(2)}) copy-start(bf16[64,1,512]{2,0,1:T(8,128)(2,1)} %copy-done.7) | copy-start | bytes 196612 | tf_op jit(solution)/shard_map/while
  51.8 84.3 %copy-start.10 = (bf16[64,1,512]{2,0,1:T(8,128)(2,1)S(1)}, bf16[64,1,512]{2,0,1:T(8,128)(2,1)}, u32[]{:S(2)}) copy-start(bf16[64,1,512]{2,0,1:T(8,128)(2,1)} %copy-done.9) | copy-start | bytes 196612 | tf_op jit(solution)/shard_map/while
  51.8 84.3 %copy-start.12 = (bf16[64,1,512]{2,0,1:T(8,128)(2,1)S(1)}, bf16[64,1,512]{2,0,1:T(8,128)(2,1)}, u32[]{:S(2)}) copy-start(bf16[64,1,512]{2,0,1:T(8,128)(2,1)} %copy-done.11) | copy-start | bytes 196612 | tf_op jit(solution)/shard_map/while
  54.2 98.9 %all-gather.9.cloned.1.call-start = ((), (), s32[]{:S(2)}) async-start(), calls=%async_computation.3 | async-start | bytes 1966080 | tf_op jit(solution)/shard_map/while/body/eval_jaxpr/all_gather | solution.py:12
  155.5 90.0 %all-reduce.6.cloned.1.call-start = ((), (), s32[]{:S(2)}) async-start(), calls=%async_computation.2 | async-start | bytes 1572864 | tf_op jit(solution)/shard_map/while/body/eval_jaxpr/psum | solution.py:45
  167.9 81.5 %copy-start.13 = (f32[1,64,512]{2,1,0:T(8,128)S(1)}, f32[1,64,512]{2,1,0:T(8,128)}, u32[]{:S(2)}) copy-start(f32[1,64,512]{2,1,0:T(8,128)} %get-tuple-element.548) | copy-start | bytes 393220 | tf_op jit(solution)/shard_map/while
  167.9 81.5 %copy-start.14 = (f32[1,64,512]{2,1,0:T(8,128)S(1)}, f32[1,64,512]{2,1,0:T(8,128)}, u32[]{:S(2)}) copy-start(f32[1,64,512]{2,1,0:T(8,128)} %get-tuple-element.549) | copy-start | bytes 393220 | tf_op jit(solution)/shard_map/while
  167.9 81.5 %copy-start.6 = (bf16[64,1,512]{2,0,1:T(8,128)(2,1)S(1)}, bf16[64,1,512]{2,0,1:T(8,128)(2,1)}, u32[]{:S(2)}) copy-start(bf16[64,1,512]{2,0,1:T(8,128)(2,1)} %copy-done.5) | copy-start | bytes 196612 | tf_op jit(solution)/shard_map/while
  167.9 81.5 %copy-start.8 = (bf16[64,1,512]{2,0,1:T(8,128)(2,1)S(1)}, bf16[64,1,512]{2,0,1:T(8,128)(2,1)}, u32[]{:S(2)}) copy-start(bf16[64,1,512]{2,0,1:T(8,128)(2,1)} %copy-done.7) | copy-start | bytes 196612 | tf_op jit(solution)/shard_map/while
  167.9 81.5 %copy-start.10 = (bf16[64,1,512]{2,0,1:T(8,128)(2,1)S(1)}, bf16[64,1,512]{2,0,1:T(8,128)(2,1)}, u32[]{:S(2)}) copy-start(bf16[64,1,512]{2,0,1:T(8,128)(2,1)} %copy-done.9) | copy-start | bytes 196612 | tf_op jit(solution)/shard_map/while
  168.0 81.5 %copy-start.12 = (bf16[64,1,512]{2,0,1:T(8,128)(2,1)S(1)}, bf16[64,1,512]{2,0,1:T(8,128)(2,1)}, u32[]{:S(2)}) copy-start(bf16[64,1,512]{2,0,1:T(8,128)(2,1)} %copy-done.11) | copy-start | bytes 196612 | tf_op jit(solution)/shard_map/while
  170.3 96.0 %all-gather.9.cloned.1.call-start = ((), (), s32[]{:S(2)}) async-start(), calls=%async_computation.3 | async-start | bytes 1966080 | tf_op jit(solution)/shard_map/while/body/eval_jaxpr/all_gather | solution.py:12
  268.7 90.1 %all-reduce.6.cloned.1.call-start = ((), (), s32[]{:S(2)}) async-start(), calls=%async_computation.2 | async-start | bytes 1572864 | tf_op jit(solution)/shard_map/while/body/eval_jaxpr/psum | solution.py:45
  281.2 81.5 %copy-start.13 = (f32[1,64,512]{2,1,0:T(8,128)S(1)}, f32[1,64,512]{2,1,0:T(8,128)}, u32[]{:S(2)}) copy-start(f32[1,64,512]{2,1,0:T(8,128)} %get-tuple-element.548) | copy-start | bytes 393220 | tf_op jit(solution)/shard_map/while
  281.2 81.5 %copy-start.14 = (f32[1,64,512]{2,1,0:T(8,128)S(1)}, f32[1,64,512]{2,1,0:T(8,128)}, u32[]{:S(2)}) copy-start(f32[1,64,512]{2,1,0:T(8,128)} %get-tuple-element.549) | copy-start | bytes 393220 | tf_op jit(solution)/shard_map/while
  281.2 81.6 %copy-start.6 = (bf16[64,1,512]{2,0,1:T(8,128)(2,1)S(1)}, bf16[64,1,512]{2,0,1:T(8,128)(2,1)}, u32[]{:S(2)}) copy-start(bf16[64,1,512]{2,0,1:T(8,128)(2,1)} %copy-done.5) | copy-start | bytes 196612 | tf_op jit(solution)/shard_map/while
  281.2 81.6 %copy-start.8 = (bf16[64,1,512]{2,0,1:T(8,128)(2,1)S(1)}, bf16[64,1,512]{2,0,1:T(8,128)(2,1)}, u32[]{:S(2)}) copy-start(bf16[64,1,512]{2,0,1:T(8,128)(2,1)} %copy-done.7) | copy-start | bytes 196612 | tf_op jit(solution)/shard_map/while
  281.2 81.6 %copy-start.10 = (bf16[64,1,512]{2,0,1:T(8,128)(2,1)S(1)}, bf16[64,1,512]{2,0,1:T(8,128)(2,1)}, u32[]{:S(2)}) copy-start(bf16[64,1,512]{2,0,1:T(8,128)(2,1)} %copy-done.9) | copy-start | bytes 196612 | tf_op jit(solution)/shard_map/while
  281.2 81.6 %copy-start.12 = (bf16[64,1,512]{2,0,1:T(8,128)(2,1)S(1)}, bf16[64,1,512]{2,0,1:T(8,128)(2,1)}, u32[]{:S(2)}) copy-start(bf16[64,1,512]{2,0,1:T(8,128)(2,1)} %copy-done.11) | copy-start | bytes 196612 | tf_op jit(solution)/shard_map/while
  283.5 96.0 %all-gather.9.cloned.1.call-start = ((), (), s32[]{:S(2)}) async-start(), calls=%async_computation.3 | async-start | bytes 1966080 | tf_op jit(solution)/shard_map/while/body/eval_jaxpr/all_gather | solution.py:12
  382.0 90.0 %all-reduce.6.cloned.1.call-start = ((), (), s32[]{:S(2)}) async-start(), calls=%async_computation.2 | async-start | bytes 1572864 | tf_op jit(solution)/shard_map/while/body/eval_jaxpr/psum | solution.py:45
  394.4 81.5 %copy-start.13 = (f32[1,64,512]{2,1,0:T(8,128)S(1)}, f32[1,64,512]{2,1,0:T(8,128)}, u32[]{:S(2)}) copy-start(f32[1,64,512]{2,1,0:T(8,128)} %get-tuple-element.548) | copy-start | bytes 393220 | tf_op jit(solution)/shard_map/while
  394.4 81.5 %copy-start.14 = (f32[1,64,512]{2,1,0:T(8,128)S(1)}, f32[1,64,512]{2,1,0:T(8,128)}, u32[]{:S(2)}) copy-start(f32[1,64,512]{2,1,0:T(8,128)} %get-tuple-element.549) | copy-start | bytes 393220 | tf_op jit(solution)/shard_map/while
  394.4 81.5 %copy-start.6 = (bf16[64,1,512]{2,0,1:T(8,128)(2,1)S(1)}, bf16[64,1,512]{2,0,1:T(8,128)(2,1)}, u32[]{:S(2)}) copy-start(bf16[64,1,512]{2,0,1:T(8,128)(2,1)} %copy-done.5) | copy-start | bytes 196612 | tf_op jit(solution)/shard_map/while
  394.4 81.5 %copy-start.8 = (bf16[64,1,512]{2,0,1:T(8,128)(2,1)S(1)}, bf16[64,1,512]{2,0,1:T(8,128)(2,1)}, u32[]{:S(2)}) copy-start(bf16[64,1,512]{2,0,1:T(8,128)(2,1)} %copy-done.7) | copy-start | bytes 196612 | tf_op jit(solution)/shard_map/while
  394.4 81.5 %copy-start.10 = (bf16[64,1,512]{2,0,1:T(8,128)(2,1)S(1)}, bf16[64,1,512]{2,0,1:T(8,128)(2,1)}, u32[]{:S(2)}) copy-start(bf16[64,1,512]{2,0,1:T(8,128)(2,1)} %copy-done.9) | copy-start | bytes 196612 | tf_op jit(solution)/shard_map/while
  394.4 81.5 %copy-start.12 = (bf16[64,1,512]{2,0,1:T(8,128)(2,1)S(1)}, bf16[64,1,512]{2,0,1:T(8,128)(2,1)}, u32[]{:S(2)}) copy-start(bf16[64,1,512]{2,0,1:T(8,128)(2,1)} %copy-done.11) | copy-start | bytes 196612 | tf_op jit(solution)/shard_map/while
  396.8 96.1 %all-gather.9.cloned.1.call-start = ((), (), s32[]{:S(2)}) async-start(), calls=%async_computation.3 | async-start | bytes 1966080 | tf_op jit(solution)/shard_map/while/body/eval_jaxpr/all_gather | solution.py:12
  495.3 90.1 %all-reduce.6.cloned.1.call-start = ((), (), s32[]{:S(2)}) async-start(), calls=%async_computation.2 | async-start | bytes 1572864 | tf_op jit(solution)/shard_map/while/body/eval_jaxpr/psum | solution.py:45
  507.8 81.5 %copy-start.13 = (f32[1,64,512]{2,1,0:T(8,128)S(1)}, f32[1,64,512]{2,1,0:T(8,128)}, u32[]{:S(2)}) copy-start(f32[1,64,512]{2,1,0:T(8,128)} %get-tuple-element.548) | copy-start | bytes 393220 | tf_op jit(solution)/shard_map/while
  507.8 81.5 %copy-start.14 = (f32[1,64,512]{2,1,0:T(8,128)S(1)}, f32[1,64,512]{2,1,0:T(8,128)}, u32[]{:S(2)}) copy-start(f32[1,64,512]{2,1,0:T(8,128)} %get-tuple-element.549) | copy-start | bytes 393220 | tf_op jit(solution)/shard_map/while
  507.8 81.6 %copy-start.6 = (bf16[64,1,512]{2,0,1:T(8,128)(2,1)S(1)}, bf16[64,1,512]{2,0,1:T(8,128)(2,1)}, u32[]{:S(2)}) copy-start(bf16[64,1,512]{2,0,1:T(8,128)(2,1)} %copy-done.5) | copy-start | bytes 196612 | tf_op jit(solution)/shard_map/while
  507.8 81.6 %copy-start.8 = (bf16[64,1,512]{2,0,1:T(8,128)(2,1)S(1)}, bf16[64,1,512]{2,0,1:T(8,128)(2,1)}, u32[]{:S(2)}) copy-start(bf16[64,1,512]{2,0,1:T(8,128)(2,1)} %copy-done.7) | copy-start | bytes 196612 | tf_op jit(solution)/shard_map/while
  507.8 81.6 %copy-start.10 = (bf16[64,1,512]{2,0,1:T(8,128)(2,1)S(1)}, bf16[64,1,512]{2,0,1:T(8,128)(2,1)}, u32[]{:S(2)}) copy-start(bf16[64,1,512]{2,0,1:T(8,128)(2,1)} %copy-done.9) | copy-start | bytes 196612 | tf_op jit(solution)/shard_map/while
  507.8 81.6 %copy-start.12 = (bf16[64,1,512]{2,0,1:T(8,128)(2,1)S(1)}, bf16[64,1,512]{2,0,1:T(8,128)(2,1)}, u32[]{:S(2)}) copy-start(bf16[64,1,512]{2,0,1:T(8,128)(2,1)} %copy-done.11) | copy-start | bytes 196612 | tf_op jit(solution)/shard_map/while
  510.2 96.0 %all-gather.9.cloned.1.call-start = ((), (), s32[]{:S(2)}) async-start(), calls=%async_computation.3 | async-start | bytes 1966080 | tf_op jit(solution)/shard_map/while/body/eval_jaxpr/all_gather | solution.py:12
  608.6 90.0 %all-reduce.6.cloned.1.call-start = ((), (), s32[]{:S(2)}) async-start(), calls=%async_computation.2 | async-start | bytes 1572864 | tf_op jit(solution)/shard_map/while/body/eval_jaxpr/psum | solution.py:45
  621.0 81.5 %copy-start.13 = (f32[1,64,512]{2,1,0:T(8,128)S(1)}, f32[1,64,512]{2,1,0:T(8,128)}, u32[]{:S(2)}) copy-start(f32[1,64,512]{2,1,0:T(8,128)} %get-tuple-element.548) | copy-start | bytes 393220 | tf_op jit(solution)/shard_map/while
  621.0 81.5 %copy-start.14 = (f32[1,64,512]{2,1,0:T(8,128)S(1)}, f32[1,64,512]{2,1,0:T(8,128)}, u32[]{:S(2)}) copy-start(f32[1,64,512]{2,1,0:T(8,128)} %get-tuple-element.549) | copy-start | bytes 393220 | tf_op jit(solution)/shard_map/while
  621.0 81.5 %copy-start.6 = (bf16[64,1,512]{2,0,1:T(8,128)(2,1)S(1)}, bf16[64,1,512]{2,0,1:T(8,128)(2,1)}, u32[]{:S(2)}) copy-start(bf16[64,1,512]{2,0,1:T(8,128)(2,1)} %copy-done.5) | copy-start | bytes 196612 | tf_op jit(solution)/shard_map/while
  621.0 81.5 %copy-start.8 = (bf16[64,1,512]{2,0,1:T(8,128)(2,1)S(1)}, bf16[64,1,512]{2,0,1:T(8,128)(2,1)}, u32[]{:S(2)}) copy-start(bf16[64,1,512]{2,0,1:T(8,128)(2,1)} %copy-done.7) | copy-start | bytes 196612 | tf_op jit(solution)/shard_map/while
  621.0 81.5 %copy-start.10 = (bf16[64,1,512]{2,0,1:T(8,128)(2,1)S(1)}, bf16[64,1,512]{2,0,1:T(8,128)(2,1)}, u32[]{:S(2)}) copy-start(bf16[64,1,512]{2,0,1:T(8,128)(2,1)} %copy-done.9) | copy-start | bytes 196612 | tf_op jit(solution)/shard_map/while
  621.1 81.5 %copy-start.12 = (bf16[64,1,512]{2,0,1:T(8,128)(2,1)S(1)}, bf16[64,1,512]{2,0,1:T(8,128)(2,1)}, u32[]{:S(2)}) copy-start(bf16[64,1,512]{2,0,1:T(8,128)(2,1)} %copy-done.11) | copy-start | bytes 196612 | tf_op jit(solution)/shard_map/while
  623.4 96.0 %all-gather.9.cloned.1.call-start = ((), (), s32[]{:S(2)}) async-start(), calls=%async_computation.3 | async-start | bytes 1966080 | tf_op jit(solution)/shard_map/while/body/eval_jaxpr/all_gather | solution.py:12
  721.8 90.1 %all-reduce.6.cloned.1.call-start = ((), (), s32[]{:S(2)}) async-start(), calls=%async_computation.2 | async-start | bytes 1572864 | tf_op jit(solution)/shard_map/while/body/eval_jaxpr/psum | solution.py:45
  734.3 81.5 %copy-start.13 = (f32[1,64,512]{2,1,0:T(8,128)S(1)}, f32[1,64,512]{2,1,0:T(8,128)}, u32[]{:S(2)}) copy-start(f32[1,64,512]{2,1,0:T(8,128)} %get-tuple-element.548) | copy-start | bytes 393220 | tf_op jit(solution)/shard_map/while
  734.3 81.5 %copy-start.14 = (f32[1,64,512]{2,1,0:T(8,128)S(1)}, f32[1,64,512]{2,1,0:T(8,128)}, u32[]{:S(2)}) copy-start(f32[1,64,512]{2,1,0:T(8,128)} %get-tuple-element.549) | copy-start | bytes 393220 | tf_op jit(solution)/shard_map/while
  734.3 81.6 %copy-start.6 = (bf16[64,1,512]{2,0,1:T(8,128)(2,1)S(1)}, bf16[64,1,512]{2,0,1:T(8,128)(2,1)}, u32[]{:S(2)}) copy-start(bf16[64,1,512]{2,0,1:T(8,128)(2,1)} %copy-done.5) | copy-start | bytes 196612 | tf_op jit(solution)/shard_map/while
  734.3 81.6 %copy-start.8 = (bf16[64,1,512]{2,0,1:T(8,128)(2,1)S(1)}, bf16[64,1,512]{2,0,1:T(8,128)(2,1)}, u32[]{:S(2)}) copy-start(bf16[64,1,512]{2,0,1:T(8,128)(2,1)} %copy-done.7) | copy-start | bytes 196612 | tf_op jit(solution)/shard_map/while
  734.3 81.6 %copy-start.10 = (bf16[64,1,512]{2,0,1:T(8,128)(2,1)S(1)}, bf16[64,1,512]{2,0,1:T(8,128)(2,1)}, u32[]{:S(2)}) copy-start(bf16[64,1,512]{2,0,1:T(8,128)(2,1)} %copy-done.9) | copy-start | bytes 196612 | tf_op jit(solution)/shard_map/while
  734.3 81.6 %copy-start.12 = (bf16[64,1,512]{2,0,1:T(8,128)(2,1)S(1)}, bf16[64,1,512]{2,0,1:T(8,128)(2,1)}, u32[]{:S(2)}) copy-start(bf16[64,1,512]{2,0,1:T(8,128)(2,1)} %copy-done.11) | copy-start | bytes 196612 | tf_op jit(solution)/shard_map/while
  736.6 96.0 %all-gather.9.cloned.1.call-start = ((), (), s32[]{:S(2)}) async-start(), calls=%async_computation.3 | async-start | bytes 1966080 | tf_op jit(solution)/shard_map/while/body/eval_jaxpr/all_gather | solution.py:12
  835.1 96.0 %all-reduce.4.cloned.1.call-start = ((), (), s32[]{:S(2)}) async-start(), calls=%async_computation | async-start | bytes 3145728 | tf_op jit(solution)/shard_map/psum | solution.py:50
  842.3 212.8 %all-gather.7.cloned.1.call-start = ((), (), s32[]{:S(2)}) async-start(), calls=%async_computation.1 | async-start | bytes 3932160 | tf_op jit(solution)/shard_map/all_gather | solution.py:12
  847.7 7.5 copy-start.17
  862.9 70.4 %copy-start.16 = (bf16[1,6,64,1024]{3,2,1,0:T(8,128)(2,1)S(1)}, bf16[1,6,64,1024]{3,2,1,0:T(8,128)(2,1)}, u32[]{:S(2)}) copy-start(bf16[1,6,64,1024]{3,2,1,0:T(8,128)(2,1)} %get-tuple-element.418) | copy-start | bytes 2359300
  1037.0 10.7 %copy-start.3 = (bf16[1,1024,4,512]{3,2,1,0:T(4,128)(2,1)S(1)}, bf16[1,1024,4,512]{3,2,1,0:T(4,128)(2,1)}, u32[]{:S(2)}) copy-start(bf16[1,1024,4,512]{3,2,1,0:T(4,128)(2,1)} %copy.23) | copy-start | bytes 12582916
  1037.0 10.7 %copy-start.4 = (bf16[1,1024,4,512]{3,2,1,0:T(4,128)(2,1)S(1)}, bf16[1,1024,4,512]{3,2,1,0:T(4,128)(2,1)}, u32[]{:S(2)}) copy-start(bf16[1,1024,4,512]{3,2,1,0:T(4,128)(2,1)} %copy.22) | copy-start | bytes 12582916
  (52 other events, 93.5 us)
Sparse Core Ops, SparseCore 0:
  54.3 77.7 all-reduce.5
  134.3 18.7 all-gather.8
  170.4 75.0 all-reduce.5
  247.5 18.7 all-gather.8
  283.7 75.0 all-reduce.5
  360.8 18.7 all-gather.8
  396.9 75.0 all-reduce.5
  474.1 18.7 all-gather.8
  510.3 75.0 all-reduce.5
  587.4 18.7 all-gather.8
  623.5 75.0 all-reduce.5
  700.6 18.7 all-gather.8
  736.8 75.0 all-reduce.5
  813.9 18.7 all-gather.8
Sparse Core Ops, SparseCore 1:
  842.4 88.7 all-reduce.3
  933.3 28.3 all-gather.6
